TPU v7x, 32 devices: a whole 2x2x4 slice. The times are simulated.
32 devices in a mesh: groups: 2 (over x), steps: 8 (over z, y), inner: 2 (over core).
Axes of the slice: x: 2, y: 2, z: 4, core: 2. Of those that a mesh axis runs over, the one named last changes fastest.
Arguments:
- start_state: float32 [16, 32, 768], P('groups'), parts along dimension 0, may hold values from -6 to 6
- noise_draws: float32 [32, 8, 32, 768], P(('groups', 'steps', 'inner')), parts along dimension 0, may hold values from -6 to 6
- step_gaps: int32 [32], P(('groups', 'steps', 'inner')), parts along dimension 0, may hold values from 1 to 15
- window_start: int32 [2], P('groups'), parts along dimension 0, may hold values from 240 to 999
- input_weight: bfloat16 [768, 1024], replicated, may hold values from -0.21875 to 0.21875
- embed_weight: bfloat16 [256, 2048], replicated, may hold values from -0.375 to 0.375
- first_weight: bfloat16 [1024, 1024], replicated, may hold values from -0.1875 to 0.1875
- second_weight: bfloat16 [1024, 1024], replicated, may hold values from -0.1875 to 0.1875
- output_weight: bfloat16 [1024, 768], replicated, may hold values from -0.1875 to 0.1875
Outputs:
- trajectory: float32 [32, 8, 32, 768], P(('groups', 'steps', 'inner')), parts along dimension 0
There are 2 independent parts, one for each index of `groups`. A program takes and returns all parts, laid end to end along the dimension named above; an argument that names none is the same for every part. Nothing has to cross between parts.
All inputs are finite; a program needn't handle non-finite values.
Results may differ from a plain program's by a relative error of at most 0.00035.
Values sent between devices are 32-bit elements; how exact they have to be, the bound alone decides.
A program may use at most 64 MiB of HBM per device.

v0:
```python
import math

import jax
import jax.numpy as jnp
from jax import lax
from jax.sharding import PartitionSpec as P

GROUPS = 32
ITERS = 2
TRAIN_STEPS = 1000


def prefix_2(part, axis, combine, identity):
    place = lax.axis_index(axis)
    gathered = lax.all_gather(part, axis)
    state = jnp.zeros_like(part) + jnp.asarray(identity, part.dtype)

    def one(turn, state):
        return combine(state, lax.dynamic_index_in_dim(gathered, turn, 0, False))

    return lax.fori_loop(0, place, one, state)


def noise_table():
    levels = jnp.arange(TRAIN_STEPS, dtype=jnp.float32)
    beta_values = 0.0001 + (0.02 - 0.0001) * levels / (TRAIN_STEPS - 1)
    return jnp.exp(jnp.cumsum(jnp.log1p(-beta_values)))


def lookup(table, noise_level):
    places = jnp.arange(TRAIN_STEPS, dtype=jnp.int32)
    return jnp.sum(jnp.where(places == noise_level, table, jnp.zeros_like(table)))


def group_norm(hidden, batch_count):
    total_rows, channel_count = hidden.shape
    shaped = hidden.reshape(batch_count, total_rows // batch_count, channel_count)

    def group_mean(values):
        per_channel = jnp.mean(values, axis=1).reshape(batch_count, GROUPS, channel_count // GROUPS)
        per_group = jnp.mean(per_channel, axis=2, keepdims=True)
        return jnp.broadcast_to(per_group, per_channel.shape).reshape(batch_count, 1, channel_count)

    center = group_mean(shaped)
    offset = shaped - center
    spread = group_mean(offset * offset)
    return (offset * lax.rsqrt(spread + 1e-05)).reshape(total_rows, channel_count)


def predict_noise(
    state, noise_level, input_weight, embed_weight, first_weight, second_weight, output_weight
):
    batch_count, patch_count, feature_count = state.shape
    channel_count = input_weight.shape[1]
    flat_state = state.reshape(batch_count * patch_count, feature_count).astype(jnp.bfloat16)
    entry_hidden = jnp.dot(flat_state, input_weight, preferred_element_type=jnp.float32)
    half_count = embed_weight.shape[0] // 2
    frequency = jnp.exp(-math.log(10000.0) * jnp.arange(half_count, dtype=jnp.float32) / half_count)
    angles = noise_level.astype(jnp.float32) * frequency
    features = jnp.concatenate([jnp.cos(angles), jnp.sin(angles)])[None, :].astype(jnp.bfloat16)
    modulation = jnp.dot(features, embed_weight, preferred_element_type=jnp.float32)
    scale_part = modulation[:, :channel_count]
    shift_part = modulation[:, channel_count:]
    act_one = jax.nn.silu(
        group_norm(entry_hidden, batch_count) * (1.0 + scale_part) + shift_part
    ).astype(jnp.bfloat16)
    middle = jnp.dot(act_one, first_weight, preferred_element_type=jnp.float32)
    act_two = jax.nn.silu(group_norm(middle, batch_count)).astype(jnp.bfloat16)
    block_out = entry_hidden + jnp.dot(act_two, second_weight, preferred_element_type=jnp.float32)
    act_three = jax.nn.silu(group_norm(block_out, batch_count)).astype(jnp.bfloat16)
    predicted = jnp.dot(act_three, output_weight, preferred_element_type=jnp.float32)
    return predicted.reshape(state.shape)


def drift_of(
    state,
    noise_draw,
    level_now,
    level_next,
    table,
    input_weight,
    embed_weight,
    first_weight,
    second_weight,
    output_weight,
):
    predicted = predict_noise(
        state, level_now, input_weight, embed_weight, first_weight, second_weight, output_weight
    )
    bar_now = lookup(table, level_now)
    bar_next = lookup(table, level_next)
    clean_guess = jnp.clip(
        (state - jnp.sqrt(1.0 - bar_now) * predicted) / jnp.sqrt(bar_now), -1.0, 1.0
    )
    implied = (state - jnp.sqrt(bar_now) * clean_guess) / jnp.sqrt(1.0 - bar_now)
    sigma_value = jnp.sqrt((1.0 - bar_next) / (1.0 - bar_now) * (1.0 - bar_now / bar_next))
    noise_coef = (1.0 - bar_next) * jnp.sqrt(bar_now / (bar_next * (1.0 - bar_now)))
    return (
        jnp.sqrt(bar_next) * clean_guess + noise_coef * implied + sigma_value * noise_draw - state
    )


def add_terms(earlier, later):
    return earlier + later


def shards(
    start_state,
    noise_draws,
    step_gaps,
    window_start,
    input_weight,
    embed_weight,
    first_weight,
    second_weight,
    output_weight,
):
    table = noise_table()
    before = prefix_2(step_gaps, ("steps", "inner"), add_terms, jnp.zeros((1,), jnp.int32))
    level_now = (window_start[0] - before[0]).astype(jnp.int32)
    level_next = level_now - step_gaps[0]
    window_count = lax.axis_size(("steps", "inner"))
    states = start_state
    drift = jnp.zeros_like(start_state)
    for iteration in range(ITERS):
        drift = drift_of(
            states,
            noise_draws[0],
            level_now,
            level_next,
            table,
            input_weight,
            embed_weight,
            first_weight,
            second_weight,
            output_weight,
        )
        blocks = drift.reshape(window_count, drift.size // window_count)
        columns = lax.all_to_all(
            blocks, ("steps", "inner"), split_axis=0, concat_axis=0, tiled=True
        )
        earlier_sums = jnp.cumsum(columns, axis=0) - columns
        returned = lax.all_to_all(
            earlier_sums, ("steps", "inner"), split_axis=0, concat_axis=0, tiled=True
        )
        prefix = returned.reshape(drift.shape)
        states = start_state + prefix
    return (states + drift)[None]


def solution(mesh):
    return jax.shard_map(
        shards,
        mesh=mesh,
        in_specs=(
            P("groups", None, None),
            P(("groups", "steps", "inner"), None, None, None),
            P(("groups", "steps", "inner")),
            P("groups"),
            P(),
            P(),
            P(),
            P(),
            P(),
        ),
        out_specs=P(("groups", "steps", "inner"), None, None, None),
        check_vma=False,
    )
```

profile of v0, /device:TPU:25, one launch (start us, length us, event | category | flops | bytes accessed | tf_op | source)
XLA Modules:
  0.0 189.5 jit_solution(16638882197625928342)
XLA Ops:
  0.8 1.2 dynamic-slice
  2.1 0.7 dynamic-update-slice
  3.4 6.5 %all-reduce.1 = s32[16]{0:T(128)S(1)} all-reduce(s32[16]{0:T(128)S(1)} %dynamic-update-slice), channel_id=2, replica_groups=mesh['groups'=2,'steps'=8,'inner'=2] {'steps','inner'}, use_global_device_ids=true, to_apply=%add.1 | all-reduce | flops 16 | bytes 128
  9.9 17.0 %while.10 = (s32[]{:T(128)}, s32[1]{0:T(128)}, s32[]{:T(128)}, s32[16,1]{0,1:T(1,128)S(1)}, s32[]{:T(128)}, /*index=5*/s32[]{:T(128)}, s32[]{:T(128)}) while((s32[]{:T(128)}, s32[1]{0:T(128)}, s32[]{:T(128)}, s32[16,1]{0,1:T(1,128)S(1)}, s32[]{:T(128)}, /*index=5*/s32[]{:T(128)}, s32[]{:T(128)}) %tuple.31), condition=%wide.region_1.2_spmd, body=%wide.region_0.0_spmd.sunk | while | flops 6 | bytes 143 | solution.py:21
  9.9 0.6 constant_dynamic-slice_fusion.2
  11.2 0.6 constant_dynamic-slice_fusion.2
  12.5 0.6 constant_dynamic-slice_fusion.2
  13.8 0.6 constant_dynamic-slice_fusion.2
  15.1 0.6 constant_dynamic-slice_fusion.2
  16.4 0.6 constant_dynamic-slice_fusion.2
  17.7 0.6 constant_dynamic-slice_fusion.2
  19.0 0.6 constant_dynamic-slice_fusion.2
  20.3 0.6 constant_dynamic-slice_fusion.2
  21.6 0.6 constant_dynamic-slice_fusion.2
  23.0 0.6 constant_dynamic-slice_fusion.2
  24.3 0.6 constant_dynamic-slice_fusion.2
  25.6 0.6 constant_dynamic-slice_fusion.2
  27.5 0.7 select_reduce_fusion
  33.5 1.6 fusion.61
  35.2 1.2 convert_element_type.39
  36.3 0.6 bitcast_reduce_fusion.3
  38.4 1.7 fusion.59
  40.5 1.4 multiply_reduce_fusion.1
  42.4 1.5 subtract_multiply_fusion.1
  44.3 1.7 bitcast_reduce_fusion.2
  46.4 1.4 fusion.42
  48.6 3.5 %fusion.52 = f32[8,32,768]{2,1,0:T(8,128)} fusion(f32[8,32,768]{2,1,0:T(8,128)} %param.11, bf16[8,32,1024]{2,1,0:T(8,128)(2,1)S(1)} %bitcast.187, bf16[1024,768]{1,0:T(8,128)(2,1)} %param.19, f32[1,8,32,768]{3,2,1,0:T(8,128)} %param.12, f32[]{:T(128)S(6)} %sqrt.28, f32[]{:T(128)S(6)} %mul.214, f32[]{:T(128)S(6)} %sqrt.12, f32[]{:T(128)S(6)} %sqrt.11, ...), kind=kOutput, calls=%fused_computation.71 | convolution fusion | flops 405209088 | bytes 4456468 | tf_op jit(solution)/shard_map/dot_general | solution.py:71
  52.1 1.9 %all_to_all.26 = f32[16,1,12288]{2,1,0:T(1,128)S(1)} reshape(f32[8,32,768]{2,1,0:T(8,128)} %fusion.52) | data formatting | bytes 1572864 | tf_op jit(solution)/shard_map/all_to_all | solution.py:139
  54.0 28.0 %all_to_all.32 = f32[16,1,12288]{2,1,0:T(1,128)S(1)} all-to-all(f32[16,1,12288]{2,1,0:T(1,128)S(1)} %all_to_all.26), channel_id=1, replica_groups=mesh['groups'=2,'steps'=8,'inner'=2] {'steps','inner'}, dimensions={0} | all-to-all | bytes 1572864 | tf_op jit(solution)/shard_map/all_to_all | solution.py:139
  82.1 0.5 reduce-window_subtract_fusion.1
  82.6 24.1 %all_to_all.33 = f32[16,1,12288]{2,1,0:T(1,128)} all-to-all(f32[16,1,12288]{2,1,0:T(1,128)S(1)} %reduce-window_subtract_fusion.1), channel_id=1, replica_groups=mesh['groups'=2,'steps'=8,'inner'=2] {'steps','inner'}, dimensions={0} | all-to-all | bytes 1572864 | tf_op jit(solution)/shard_map/all_to_all | solution.py:143
  106.7 3.9 %reduce.1 = f32[16,12288]{1,0:T(8,128)} reduce(f32[16,1,12288]{2,1,0:T(1,128)} %all_to_all.33, f32[]{:T(128)} %constant.96), dimensions={1}, to_apply=%all_to_all.22.reduce_sub_computation | reduce | bytes 1572868 | tf_op jit(solution)/shard_map/all_to_all | solution.py:143
  110.6 2.1 %reshape.285 = f32[8,32,768]{2,1,0:T(8,128)} reshape(f32[16,12288]{1,0:T(8,128)} %reduce.1) | data formatting | bytes 1572864 | tf_op jit(solution)/shard_map/reshape | solution.py:146
  112.7 2.2 %fusion.58 = (bf16[8,32,768]{2,1,0:T(8,128)(2,1)S(1)}, f32[8,32,768]{2,1,0:T(8,128)}) fusion(f32[8,32,768]{2,1,0:T(8,128)S(1)} %copy-done.5, f32[8,32,768]{2,1,0:T(8,128)} %reshape.285), kind=kLoop, calls=%fused_computation.112 | loop fusion | flops 393216 | bytes 2752512 | tf_op jit(solution)/shard_map/convert_element_type | solution.py:55
  115.0 0.6 bitcast_reduce_fusion.1
  117.0 1.7 fusion.60
  119.1 1.4 multiply_reduce_fusion
  121.0 1.5 subtract_multiply_fusion
  122.9 1.7 bitcast_reduce_fusion
  125.0 1.4 fusion.33
  127.2 3.5 %fusion.53 = f32[8,32,768]{2,1,0:T(8,128)} fusion(f32[8,32,768]{2,1,0:T(8,128)} %get-tuple-element.40, bf16[8,32,1024]{2,1,0:T(8,128)(2,1)S(1)} %bitcast.186, bf16[1024,768]{1,0:T(8,128)(2,1)} %param.19, f32[1,8,32,768]{3,2,1,0:T(8,128)} %param.12, f32[]{:T(128)S(6)} %sqrt.28, f32[]{:T(128)S(6)} %mul.214, f32[]{:T(128)S(6)} %sqrt.12, f32[]{:T(128)S(6)} %sqrt.11, ...), kind=kOutput, calls=%fused_computation.72 | convolution fusion | flops 405209088 | bytes 4456468 | tf_op jit(solution)/shard_map/dot_general | solution.py:71
  130.7 1.9 %all_to_all.27 = f32[16,1,12288]{2,1,0:T(1,128)S(1)} reshape(f32[8,32,768]{2,1,0:T(8,128)} %fusion.53) | data formatting | bytes 1572864 | tf_op jit(solution)/shard_map/all_to_all | solution.py:139
  132.6 23.9 %all_to_all.34 = f32[16,1,12288]{2,1,0:T(1,128)S(1)} all-to-all(f32[16,1,12288]{2,1,0:T(1,128)S(1)} %all_to_all.27), channel_id=1, replica_groups=mesh['groups'=2,'steps'=8,'inner'=2] {'steps','inner'}, dimensions={0} | all-to-all | bytes 1572864 | tf_op jit(solution)/shard_map/all_to_all | solution.py:139
  156.5 0.5 reduce-window_subtract_fusion
  157.0 24.1 %all_to_all.35 = f32[16,1,12288]{2,1,0:T(1,128)} all-to-all(f32[16,1,12288]{2,1,0:T(1,128)S(1)} %reduce-window_subtract_fusion), channel_id=1, replica_groups=mesh['groups'=2,'steps'=8,'inner'=2] {'steps','inner'}, dimensions={0} | all-to-all | bytes 1572864 | tf_op jit(solution)/shard_map/all_to_all | solution.py:143
  181.1 3.9 %reduce.2 = f32[16,12288]{1,0:T(8,128)} reduce(f32[16,1,12288]{2,1,0:T(1,128)} %all_to_all.35, f32[]{:T(128)} %constant.96), dimensions={1}, to_apply=%all_to_all.25.reduce_sub_computation | reduce | bytes 1572868 | tf_op jit(solution)/shard_map/all_to_all | solution.py:143
  185.0 2.2 %reshape.289 = f32[8,32,768]{2,1,0:T(8,128)} reshape(f32[16,12288]{1,0:T(8,128)} %reduce.2) | data formatting | bytes 1572864 | tf_op jit(solution)/shard_map/reshape | solution.py:146
  187.1 2.4 %add_bitcast_fusion = f32[1,8,32,768]{3,2,1,0:T(8,128)} fusion(f32[8,32,768]{2,1,0:T(8,128)} %fusion.53, f32[8,32,768]{2,1,0:T(8,128)S(1)} %copy-done.6, f32[8,32,768]{2,1,0:T(8,128)} %reshape.289), kind=kLoop, calls=%fused_computation.73 | loop fusion | flops 393216 | bytes 3145728 | tf_op jit(solution)/shard_map/broadcast_in_dim | solution.py:148
  (110 shorter events, 8.0 us)
Async XLA Ops:
  0.0 38.3 %copy-start = (bf16[1024,1024]{1,0:T(8,128)(2,1)S(1)}, bf16[1024,1024]{1,0:T(8,128)(2,1)}, u32[]{:S(2)}) copy-start(bf16[1024,1024]{1,0:T(8,128)(2,1)} %param.17) | copy-start | bytes 6291460
  33.5 2.8 %copy-start.7 = (bf16[768,1024]{1,0:T(8,128)(2,1)S(1)}, bf16[768,1024]{1,0:T(8,128)(2,1)}, u32[]{:S(2)}) copy-start(bf16[768,1024]{1,0:T(8,128)(2,1)} %param.15) | copy-start | bytes 4718596
  42.4 1.9 %copy-start.3 = (bf16[1024,1024]{1,0:T(8,128)(2,1)S(1)}, bf16[1024,1024]{1,0:T(8,128)(2,1)}, u32[]{:S(2)}) copy-start(bf16[1024,1024]{1,0:T(8,128)(2,1)} %param.18) | copy-start | bytes 6291460
  46.0 2.3 %copy-start.2 = (f32[256,1024]{1,0:T(8,128)S(1)}, f32[256,1024]{1,0:T(8,128)}, u32[]{:S(2)}) copy-start(f32[256,1024]{1,0:T(8,128)} %get-tuple-element.48) | copy-start | bytes 3145732
  82.6 30.1 %copy-start.5 = (f32[8,32,768]{2,1,0:T(8,128)S(1)}, f32[8,32,768]{2,1,0:T(8,128)}, u32[]{:S(2)}) copy-start(f32[8,32,768]{2,1,0:T(8,128)} %param.11) | copy-start | bytes 2359300
  112.7 2.2 %copy-start.8 = (bf16[768,1024]{1,0:T(8,128)(2,1)S(1)}, bf16[768,1024]{1,0:T(8,128)(2,1)}, u32[]{:S(2)}) copy-start(bf16[768,1024]{1,0:T(8,128)(2,1)} %param.15) | copy-start | bytes 4718596
  121.0 1.9 %copy-start.4 = (bf16[1024,1024]{1,0:T(8,128)(2,1)S(1)}, bf16[1024,1024]{1,0:T(8,128)(2,1)}, u32[]{:S(2)}) copy-start(bf16[1024,1024]{1,0:T(8,128)(2,1)} %param.18) | copy-start | bytes 6291460
  124.6 2.3 %copy-start.1 = (f32[256,1024]{1,0:T(8,128)S(1)}, f32[256,1024]{1,0:T(8,128)}, u32[]{:S(2)}) copy-start(f32[256,1024]{1,0:T(8,128)} %get-tuple-element.54) | copy-start | bytes 3145732
  157.0 30.1 %copy-start.6 = (f32[8,32,768]{2,1,0:T(8,128)S(1)}, f32[8,32,768]{2,1,0:T(8,128)}, u32[]{:S(2)}) copy-start(f32[8,32,768]{2,1,0:T(8,128)} %param.11) | copy-start | bytes 2359300
where the time goes:
time: 193 us; the launch traced here: 190 us
  blocking collectives  107 us (55%)
  other arithmetic  28 us (15%)
  local copies, waits for them, and re-layouts  22.5 us (12%)
  matrix products  16.6 us (9%)
  loops' own time  8.54 us (4%)
  between operations  7.39 us (4%)
    all_to_all x2, blocking collectives, shards(): lax.all_to_all(blocks, ('steps', 'inner'), split_axis=0, concat_axis=0, t...  51.9 us
    all_to_all x2, blocking collectives, shards(): lax.all_to_all(earlier_sums, ('steps', 'inner'), split_axis=0, concat_axi...  48.2 us
    another operation x1, loops' own time, prefix_2(): return lax.fori_loop(0, place, one, state)  8.54 us
    dynamic_slice x13, local copies, waits for them, and re-layouts, one(): return combine(state, lax.dynamic_index_in_dim(gathered, turn, 0, False))  8.43 us
    all_to_all x2, other arithmetic, shards(): lax.all_to_all(earlier_sums, ('steps', 'inner'), split_axis=0, concat_axi...  7.77 us
    dot_general x2, matrix products, predict_noise(): jnp.dot(act_three, output_weight, preferred_element_type=jnp.float32)  6.95 us
    unnamed x1, blocking collectives  6.51 us
    reduce_sum x6, other arithmetic, group_mean(): jnp.mean(values, axis=1)  5.97 us

commit v1 on v0

v1 whole, which is shorter than its diff:
```python
import functools
import math

import jax
import jax.numpy as jnp
import numpy as np
from jax import lax
from jax.experimental import pallas as pl
from jax.experimental.pallas import tpu as pltpu
from jax.sharding import PartitionSpec as P

GROUPS = 32
ITERS = 2
TRAIN_STEPS = 1000
CHUNK_IMAGES = 2
LANES = 128
BLOCK = 256
MESH = pl.DeviceIdType.MESH
F32 = jnp.float32
BF16 = jnp.bfloat16


def noise_table():
    levels = np.arange(TRAIN_STEPS, dtype=np.float32)
    beta = (0.0001 + (0.02 - 0.0001) * levels / (TRAIN_STEPS - 1)).astype(np.float32)
    bars = np.exp(np.cumsum(np.log1p(-beta.astype(np.float64)))).astype(np.float32)
    padded = np.zeros((-(-TRAIN_STEPS // (8 * LANES)) * 8 * LANES,), np.float32)
    padded[:TRAIN_STEPS] = bars
    return padded.reshape(-1, LANES)


def frequencies(count):
    powers = -math.log(10000.0) * np.arange(count, dtype=np.float32) / count
    return np.exp(powers.astype(np.float32)).astype(np.float32)[None, :]


def group_matrix(channels, rows):
    width = channels // GROUPS
    place = np.arange(BLOCK) // width
    same = (place[:, None] == place[None, :]).astype(np.float32)
    return same / (width * rows)


def silu(value):
    half = 0.5 * value
    return half + half * jnp.tanh(half)


def kernel(
    cfg,
    gap_ref,
    start_level_ref,
    table_ref,
    freq_ref,
    group_ref,
    start_hbm,
    noise_hbm,
    win_hbm,
    wemb_hbm,
    w1_hbm,
    w2_hbm,
    wout_hbm,
    out_hbm,
    start_v,
    noise_v,
    win,
    wemb,
    w1,
    w2,
    wout,
    gap_send,
    gap_all,
    modulation_v,
    coef_v,
    drift_v,
    core_rx,
    chain_rx,
    chain_tx,
    side_rx,
    final_tx,
    prefix_v,
    out_v,
    load_sem,
    gap_send_sem,
    gap_recv_sem,
    core_send,
    core_recv,
    chain_send,
    chain_recv,
    side_send,
    side_recv,
    final_send,
    final_recv,
    out_sem,
):
    steps, inner, columns, chunks, size, patches, features, channels = cfg
    rows = steps // columns
    half = size // 2
    total = size * patches
    s = lax.axis_index("steps")
    h = lax.axis_index("inner")
    z, y = s // columns, lax.rem(s, columns)
    window = steps * inner
    me = s * inner + h
    messages = ITERS * chunks

    loads = [
        pltpu.make_async_copy(src, dst, load_sem.at[i])
        for i, (src, dst) in enumerate(
            [
                (start_hbm, start_v),
                (win_hbm, win),
                (wemb_hbm, wemb),
                (w1_hbm, w1),
                (w2_hbm, w2),
                (wout_hbm, wout),
                (noise_hbm, noise_v),
            ]
        )
    ]
    for load in loads:
        load.start()
    gap_send[...] = jnp.zeros_like(gap_send) + gap_ref[0]

    barrier = pltpu.get_barrier_semaphore()
    for j in range(1, window):
        to = lax.rem(me + j, window)
        pl.semaphore_signal(
            barrier,
            inc=1,
            device_id={"steps": to // inner, "inner": lax.rem(to, inner)},
            device_id_type=MESH,
        )
    pl.semaphore_wait(barrier, window - 1)

    def gap_copy(j):
        to = lax.rem(me + j, window)
        return pltpu.make_async_remote_copy(
            src_ref=gap_send,
            dst_ref=gap_all.at[me],
            send_sem=gap_send_sem.at[j],
            recv_sem=gap_recv_sem.at[me],
            device_id={"steps": to // inner, "inner": lax.rem(to, inner)},
            device_id_type=MESH,
        )

    def gap_arrival(j):
        origin = lax.rem(me + j, window)
        return pltpu.make_async_remote_copy(
            src_ref=gap_send,
            dst_ref=gap_all.at[origin],
            send_sem=gap_send_sem.at[j],
            recv_sem=gap_recv_sem.at[origin],
            device_id={"steps": origin // inner, "inner": lax.rem(origin, inner)},
            device_id_type=MESH,
        )

    for j in range(1, window):
        gap_copy(j).start()

    for n in range(chunks):
        prefix_v[n] = jnp.zeros(prefix_v.shape[1:], F32)

    @pl.when(z == 0)
    def _():
        chain_rx[...] = jnp.zeros_like(chain_rx)

    def core_copy(m):
        return pltpu.make_async_remote_copy(
            src_ref=drift_v.at[m, 1 - h],
            dst_ref=core_rx.at[m],
            send_sem=core_send.at[m],
            recv_sem=core_recv.at[m],
            device_id={"inner": 1 - h},
            device_id_type=MESH,
        )

    def chain_copy(m):
        return pltpu.make_async_remote_copy(
            src_ref=chain_tx.at[m],
            dst_ref=chain_rx.at[m],
            send_sem=chain_send.at[m],
            recv_sem=chain_recv.at[m],
            device_id={"steps": lax.rem(s + columns, steps)},
            device_id_type=MESH,
        )

    def side_copy(m, source):
        return pltpu.make_async_remote_copy(
            src_ref=source.at[m],
            dst_ref=side_rx.at[m],
            send_sem=side_send.at[m],
            recv_sem=side_recv.at[m],
            device_id={"steps": z * columns + (1 - y)},
            device_id_type=MESH,
        )

    def final_copy(m):
        return pltpu.make_async_remote_copy(
            src_ref=final_tx.at[m],
            dst_ref=prefix_v.at[m + chunks, h],
            send_sem=final_send.at[m],
            recv_sem=final_recv.at[m],
            device_id={"inner": 1 - h},
            device_id_type=MESH,
        )

    def final_arrival(m):
        return pltpu.make_async_remote_copy(
            src_ref=final_tx.at[m],
            dst_ref=prefix_v.at[m + chunks, 1 - h],
            send_sem=final_send.at[m],
            recv_sem=final_recv.at[m],
            device_id={"inner": 1 - h},
            device_id_type=MESH,
        )

    def out_copy(c):
        return pltpu.make_async_copy(out_v.at[c], out_hbm.at[c], out_sem.at[c])

    def chain(m):
        core_copy(m).wait_recv()

        @pl.when(z > 0)
        def _():
            chain_copy(m).wait_recv()

        chain_tx[m] = chain_rx[m] + (drift_v[m, h] + core_rx[m])

        @pl.when(z < rows - 1)
        def _():
            chain_copy(m).start()

        if columns == 2:

            @pl.when(y == 0)
            def _():
                side_copy(m, chain_tx).start()

            @pl.when(y == 1)
            def _():
                side_copy(m, chain_rx).start()

    def hand_back(m):
        prefix = chain_rx[m]
        if columns == 2:
            side_copy(m, chain_tx).wait_recv()
            prefix = prefix + side_rx[m]

        @pl.when(h == 0)
        def _():
            final_tx[m] = prefix + drift_v[m, 0]
            prefix_v[m + chunks, 0] = prefix

        @pl.when(h == 1)
        def _():
            final_tx[m] = prefix
            prefix_v[m + chunks, 1] = prefix + core_rx[m]

        final_copy(m).start()

    def finish(m):
        final_arrival(m).wait_recv()

    def group_average(partial):
        blocks = channels // BLOCK
        stacked = jnp.concatenate(
            [partial[:, i * BLOCK : (i + 1) * BLOCK] for i in range(blocks)], axis=0
        )
        matrix = group_ref[...]
        high = stacked.astype(BF16)
        rest = stacked - high.astype(F32)
        middle = rest.astype(BF16)
        low = (rest - middle.astype(F32)).astype(BF16)
        summed = (
            jnp.dot(low, matrix, preferred_element_type=F32)
            + jnp.dot(middle, matrix, preferred_element_type=F32)
            + jnp.dot(high, matrix, preferred_element_type=F32)
        )
        summed = jnp.sum(summed.reshape(blocks, size, 8, BLOCK), axis=2, keepdims=True)
        return jnp.concatenate([summed[i] for i in range(blocks)], axis=-1)

    def row_sums(value):
        return jnp.sum(value.reshape(size, patches // 8, 8, channels), axis=1).reshape(
            size * 8, channels
        )

    def centered(hidden):
        shaped = hidden.reshape(size, patches, channels)
        offset = shaped - group_average(row_sums(shaped))
        return offset, lax.rsqrt(group_average(row_sums(offset * offset)) + 1e-05)

    def set_level():
        for j in range(1, window):
            gap_arrival(j).wait_recv()
        earlier = jnp.zeros(gap_send.shape, jnp.int32)
        for k in range(window):
            earlier = earlier + jnp.where(k < me, gap_all[k], 0)
        level_now = start_level_ref[0] - earlier
        level_next = level_now - gap_ref[0]
        table = table_ref[...]
        places = lax.broadcasted_iota(jnp.int32, table.shape, 0) * LANES + (
            lax.broadcasted_iota(jnp.int32, table.shape, 1)
        )

        def lookup(level):
            found = jnp.where(places == level[:1, :1], table, 0.0)
            return jnp.sum(jnp.sum(found, axis=0, keepdims=True), axis=1, keepdims=True)

        bar_now, bar_next = lookup(level_now), lookup(level_next)
        coefs = [
            jnp.sqrt(1.0 - bar_now),
            1.0 / jnp.sqrt(bar_now),
            jnp.sqrt(bar_now),
            1.0 / jnp.sqrt(1.0 - bar_now),
            jnp.sqrt(bar_next),
            (1.0 - bar_next) * jnp.sqrt(bar_now / (bar_next * (1.0 - bar_now))),
            jnp.sqrt((1.0 - bar_next) / (1.0 - bar_now) * (1.0 - bar_now / bar_next)),
        ]
        for i, coef in enumerate(coefs):
            coef_v[i] = jnp.broadcast_to(coef, coef_v.shape[1:])
        angles = level_now.astype(F32)[:, :1] * freq_ref[...]
        around = jnp.concatenate([jnp.cos(angles), jnp.sin(angles)], axis=1).astype(BF16)
        loads[2].wait()
        modulation_v[...] = jnp.dot(around, wemb[...], preferred_element_type=F32)

    def compute(n):
        c = lax.rem(n, chunks)

        @pl.when(n == 0)
        def _():
            loads[0].wait()
            loads[1].wait()

        state = start_v[c] + prefix_v[n].reshape(size, patches, features)
        flat = state.reshape(total, features).astype(BF16)
        entry = jnp.dot(flat, win[...], preferred_element_type=F32)
        offset, spread = centered(entry)

        @pl.when(n == 0)
        def _():
            set_level()
            loads[3].wait()

        scale = modulation_v[:1, :channels].reshape(1, 1, channels)
        shift = modulation_v[:1, channels:].reshape(1, 1, channels)
        one = silu(offset * (spread * (1.0 + scale)) + shift).astype(BF16)
        middle = jnp.dot(one.reshape(total, channels), w1[...], preferred_element_type=F32)
        offset, spread = centered(middle)
        two = silu(offset * spread).astype(BF16)

        @pl.when(n == 0)
        def _():
            loads[4].wait()

        block = entry + jnp.dot(
            two.reshape(total, channels), w2[...], preferred_element_type=F32
        )
        offset, spread = centered(block)
        three = silu(offset * spread).astype(BF16)

        @pl.when(n == 0)
        def _():
            loads[5].wait()
            loads[6].wait()

        eps = jnp.dot(three.reshape(total, channels), wout[...], preferred_element_type=F32)
        eps = eps.reshape(size, patches, features)
        state = start_v[c] + prefix_v[n].reshape(size, patches, features)
        coef = [coef_v[i][:1, :1].reshape(1, 1, 1) for i in range(7)]
        clean = jnp.clip((state - coef[0] * eps) * coef[1], -1.0, 1.0)
        implied = (state - coef[2] * clean) * coef[3]
        drift = coef[4] * clean + coef[5] * implied + coef[6] * noise_v[c] - state
        drift_v[n] = drift.reshape(2, half, patches, features)
        core_copy(n).start()

    def step(n, carry):
        @pl.when(n >= chunks)
        def _():
            finish(n - chunks)

        compute(n)

        @pl.when(n >= 1)
        def _():
            chain(n - 1)

        @pl.when(n >= chunks - 1)
        def _():
            hand_back(n - chunks + 1)

        return carry

    lax.fori_loop(0, messages, step, 0)

    def emit(m):
        finish(m)
        c = m - (ITERS - 1) * chunks
        whole = prefix_v[m + chunks] + drift_v[m]
        out_v[c] = start_v[c] + whole.reshape(size, patches, features)
        out_copy(c).start()

    chain(messages - 1)
    for m in range(messages - chunks + 1, messages):
        hand_back(m)
        emit(m - 1)
    emit(messages - 1)

    for j in range(1, window):
        gap_copy(j).wait_send()
    for m in range(messages):
        core_copy(m).wait_send()
        final_copy(m).wait_send()
        if columns == 2:
            side_copy(m, chain_tx).wait_send()

    @pl.when(z < rows - 1)
    def _():
        for m in range(messages):
            chain_copy(m).wait_send()

    for c in range(chunks):
        out_copy(c).wait()


def shards(
    steps,
    inner,
    start_state,
    noise_draws,
    step_gaps,
    window_start,
    input_weight,
    embed_weight,
    first_weight,
    second_weight,
    output_weight,
):
    batch, patches, features = start_state.shape
    channels = input_weight.shape[1]
    size = CHUNK_IMAGES
    half, chunks = size // 2, batch // size
    columns = 2 if steps % 2 == 0 else 1
    window = steps * inner
    messages = ITERS * chunks
    chunked = (chunks, size, patches, features)
    piece = (messages, half, patches, features)
    cfg = (steps, inner, columns, chunks, size, patches, features, channels)
    table = jnp.asarray(noise_table())
    freq = jnp.asarray(frequencies(embed_weight.shape[0] // 2))
    matrix = jnp.asarray(group_matrix(channels, patches)).astype(BF16)
    smem = pl.BlockSpec(memory_space=pltpu.SMEM)
    vmem = pl.BlockSpec(memory_space=pltpu.VMEM)
    anywhere = pl.BlockSpec(memory_space=pl.ANY)
    dma = pltpu.SemaphoreType.DMA
    out = pl.pallas_call(
        functools.partial(kernel, cfg),
        out_shape=jax.ShapeDtypeStruct(chunked, F32),
        in_specs=[smem, smem, vmem, vmem, vmem] + [anywhere] * 7,
        out_specs=anywhere,
        scratch_shapes=[
            pltpu.VMEM(chunked, F32),
            pltpu.VMEM(chunked, F32),
            pltpu.VMEM(input_weight.shape, BF16),
            pltpu.VMEM(embed_weight.shape, BF16),
            pltpu.VMEM(first_weight.shape, BF16),
            pltpu.VMEM(second_weight.shape, BF16),
            pltpu.VMEM(output_weight.shape, BF16),
            pltpu.VMEM((8, LANES), jnp.int32),
            pltpu.VMEM((window, 8, LANES), jnp.int32),
            pltpu.VMEM((8, 2 * channels), F32),
            pltpu.VMEM((7, 8, LANES), F32),
            pltpu.VMEM((messages, 2, half, patches, features), F32),
            pltpu.VMEM(piece, F32),
            pltpu.VMEM(piece, F32),
            pltpu.VMEM(piece, F32),
            pltpu.VMEM(piece, F32),
            pltpu.VMEM(piece, F32),
            pltpu.VMEM((messages + chunks, 2, half, patches, features), F32),
            pltpu.VMEM(chunked, F32),
            dma((7,)),
            dma((window,)),
            dma((window,)),
        ]
        + [dma((messages,))] * 8
        + [dma((chunks,))],
        compiler_params=pltpu.CompilerParams(
            collective_id=0, has_side_effects=True, vmem_limit_bytes=56 * 1024 * 1024
        ),
    )(
        step_gaps,
        window_start,
        table,
        freq,
        matrix,
        start_state.reshape(chunked),
        noise_draws.reshape(chunked),
        input_weight,
        embed_weight,
        first_weight,
        second_weight,
        output_weight,
    )
    return out.reshape((1,) + start_state.shape)


def solution(mesh):
    steps, inner = mesh.shape["steps"], mesh.shape["inner"]
    return jax.shard_map(
        functools.partial(shards, steps, inner),
        mesh=mesh,
        in_specs=(
            P("groups", None, None),
            P(("groups", "steps", "inner"), None, None, None),
            P(("groups", "steps", "inner")),
            P("groups"),
            P(),
            P(),
            P(),
            P(),
            P(),
        ),
        out_specs=P(("groups", "steps", "inner"), None, None, None),
        check_vma=False,
    )
```

time: 193 us -> 63.1 us (0.33); the launches traced: 190 us -> 62.9 us
  blocking collectives: 107 us -> 0 us
  Pallas kernels: 0 us -> 59.5 us
  other arithmetic: 28 us -> 0 us
  local copies, waits for them, and re-layouts: 22.5 us -> 2.07 us
  matrix products: 16.6 us -> 0 us
  loops' own time: 8.54 us -> 0 us
  between operations: 7.39 us -> 1.3 us
    all_to_all x4 -> x0, blocking collectives: 100 us -> none  [the longest x2 51.9 us: shards(): lax.all_to_all(blocks, ('steps', 'inner'), split_axis=0, concat_axis=0, t...]
    pallas_call x0 -> x1, Pallas kernels: none -> 59.5 us  [shards(): pl.pallas_call(functools.partial(kernel, cfg), out_shape=jax.ShapeDtypeSt...]
    dot_general x9 -> x0, matrix products: 16.6 us -> none  [the longest x2 6.95 us: predict_noise(): jnp.dot(act_three, output_weight, preferred_element_type=jnp.float32)]
    another operation x1 -> x0, loops' own time: 8.54 us -> none  [prefix_2(): return lax.fori_loop(0, place, one, state)]
    dynamic_slice x13 -> x0, local copies, waits for them, and re-layouts: 8.43 us -> none  [one(): return combine(state, lax.dynamic_index_in_dim(gathered, turn, 0, False))]
    reduce_sum x19 -> x0, other arithmetic: 7.93 us -> none  [the longest x6 5.97 us: group_mean(): jnp.mean(values, axis=1)]
    all_to_all x2 -> x0, other arithmetic: 7.77 us -> none  [shards(): lax.all_to_all(earlier_sums, ('steps', 'inner'), split_axis=0, concat_axi...]
    unnamed x1 -> x0, blocking collectives: 6.51 us -> none
where the time goes in v1:
time: 63.1 us; the launch traced here: 62.9 us
  Pallas kernels  59.5 us (94%)
  local copies, waits for them, and re-layouts  2.07 us (3%)
  between operations  1.3 us (2%)
    pallas_call x1, Pallas kernels, shards(): pl.pallas_call(functools.partial(kernel, cfg), out_shape=jax.ShapeDtypeSt...  59.5 us
    unnamed x1, local copies, waits for them, and re-layouts  2.07 us

profile of v1, /device:TPU:25, one launch (start us, length us, event | category | flops | bytes accessed | tf_op | source)
XLA Modules:
  0.0 62.9 jit_solution(2796418313542722620)
XLA Ops:
  1.3 59.5 %shard_map.118 = f32[4,2,32,768]{3,2,1,0:T(8,128)} custom-call(s32[1]{0:T(128)S(6)} %copy.14.gap_ref, s32[1]{0:T(128)S(6)} %copy.15.start_level_ref, f32[8,128]{1,0:T(8,128)} %constant.6.clone.table_ref, f32[1,128]{1,0:T(1,128)} %constant.7.clone.freq_ref, bf16[256,256]{1,0:T(8,128)(2,1)} %constant.12.group_ref, f32[4,2,32,768]{3,2,1,0:T(8,128)} %bitcast.4, ...), custom_call_target="tpu_custom_call" | custom-call | tf_op jit(solution)/shard_map/pallas_call | solution.py:456
  60.8 2.1 %copy.16 = f32[1,8,32,768]{3,2,1,0:T(8,128)} copy(f32[1,8,32,768]{3,2,1,0:T(8,128)} %bitcast.3) | data formatting | bytes 1572864

commit v2 on v1

--- a/solution.py
+++ b/solution.py
@@ -10,6 +10,7 @@
 from jax.sharding import PartitionSpec as P
 
 GROUPS = 32
+PIECES = 2
 ITERS = 2
 TRAIN_STEPS = 1000
 CHUNK_IMAGES = 2
@@ -60,7 +61,7 @@
     w1_hbm,
     w2_hbm,
     wout_hbm,
-    out_hbm,
+    out_v,
     start_v,
     noise_v,
     win,
@@ -79,7 +80,6 @@
     side_rx,
     final_tx,
     prefix_v,
-    out_v,
     load_sem,
     gap_send_sem,
     gap_recv_sem,
@@ -91,7 +91,6 @@
     side_recv,
     final_send,
     final_recv,
-    out_sem,
 ):
     steps, inner, columns, chunks, size, patches, features, channels = cfg
     rows = steps // columns
@@ -175,22 +174,27 @@
             device_id_type=MESH,
         )
 
-    def chain_copy(m):
-        return pltpu.make_async_remote_copy(
-            src_ref=chain_tx.at[m],
-            dst_ref=chain_rx.at[m],
-            send_sem=chain_send.at[m],
-            recv_sem=chain_recv.at[m],
+    depth = patches // PIECES
+
+    def part(ref, m, q):
+        return ref.at[m, :, q * depth : (q + 1) * depth]
+
+    def chain_copy(m, q):
+        return pltpu.make_async_remote_copy(
+            src_ref=part(chain_tx, m, q),
+            dst_ref=part(chain_rx, m, q),
+            send_sem=chain_send.at[m, q],
+            recv_sem=chain_recv.at[m, q],
             device_id={"steps": lax.rem(s + columns, steps)},
             device_id_type=MESH,
         )
 
-    def side_copy(m, source):
-        return pltpu.make_async_remote_copy(
-            src_ref=source.at[m],
-            dst_ref=side_rx.at[m],
-            send_sem=side_send.at[m],
-            recv_sem=side_recv.at[m],
+    def side_copy(m, source, q):
+        return pltpu.make_async_remote_copy(
+            src_ref=part(source, m, q),
+            dst_ref=part(side_rx, m, q),
+            send_sem=side_send.at[m, q],
+            recv_sem=side_recv.at[m, q],
             device_id={"steps": z * columns + (1 - y)},
             device_id_type=MESH,
         )
@@ -215,36 +219,36 @@
             device_id_type=MESH,
         )
 
-    def out_copy(c):
-        return pltpu.make_async_copy(out_v.at[c], out_hbm.at[c], out_sem.at[c])
-
     def chain(m):
         core_copy(m).wait_recv()
-
-        @pl.when(z > 0)
-        def _():
-            chain_copy(m).wait_recv()
-
-        chain_tx[m] = chain_rx[m] + (drift_v[m, h] + core_rx[m])
-
-        @pl.when(z < rows - 1)
-        def _():
-            chain_copy(m).start()
-
-        if columns == 2:
-
-            @pl.when(y == 0)
+        for q in range(PIECES):
+            cut = slice(q * depth, (q + 1) * depth)
+
+            @pl.when(z > 0)
             def _():
-                side_copy(m, chain_tx).start()
-
-            @pl.when(y == 1)
+                chain_copy(m, q).wait_recv()
+
+            chain_tx[m, :, cut] = chain_rx[m, :, cut] + (drift_v[m, h, :, cut] + core_rx[m, :, cut])
+
+            @pl.when(z < rows - 1)
             def _():
-                side_copy(m, chain_rx).start()
+                chain_copy(m, q).start()
+
+            if columns == 2:
+
+                @pl.when(y == 0)
+                def _():
+                    side_copy(m, chain_tx, q).start()
+
+                @pl.when(y == 1)
+                def _():
+                    side_copy(m, chain_rx, q).start()
 
     def hand_back(m):
         prefix = chain_rx[m]
         if columns == 2:
-            side_copy(m, chain_tx).wait_recv()
+            for q in range(PIECES):
+                side_copy(m, chain_tx, q).wait_recv()
             prefix = prefix + side_rx[m]
 
         @pl.when(h == 0)
@@ -327,20 +331,10 @@
     def compute(n):
         c = lax.rem(n, chunks)
 
-        @pl.when(n == 0)
-        def _():
-            loads[0].wait()
-            loads[1].wait()
-
         state = start_v[c] + prefix_v[n].reshape(size, patches, features)
         flat = state.reshape(total, features).astype(BF16)
         entry = jnp.dot(flat, win[...], preferred_element_type=F32)
         offset, spread = centered(entry)
-
-        @pl.when(n == 0)
-        def _():
-            set_level()
-            loads[3].wait()
 
         scale = modulation_v[:1, :channels].reshape(1, 1, channels)
         shift = modulation_v[:1, channels:].reshape(1, 1, channels)
@@ -349,20 +343,15 @@
         offset, spread = centered(middle)
         two = silu(offset * spread).astype(BF16)
 
-        @pl.when(n == 0)
+        @pl.when(n >= chunks - 1)
         def _():
-            loads[4].wait()
+            hand_back(n - chunks + 1)
 
         block = entry + jnp.dot(
             two.reshape(total, channels), w2[...], preferred_element_type=F32
         )
         offset, spread = centered(block)
         three = silu(offset * spread).astype(BF16)
-
-        @pl.when(n == 0)
-        def _():
-            loads[5].wait()
-            loads[6].wait()
 
         eps = jnp.dot(three.reshape(total, channels), wout[...], preferred_element_type=F32)
         eps = eps.reshape(size, patches, features)
@@ -385,12 +374,11 @@
         def _():
             chain(n - 1)
 
-        @pl.when(n >= chunks - 1)
-        def _():
-            hand_back(n - chunks + 1)
-
         return carry
 
+    for i in (0, 1, 3, 4, 5, 6):
+        loads[i].wait()
+    set_level()
     lax.fori_loop(0, messages, step, 0)
 
     def emit(m):
@@ -398,7 +386,6 @@
         c = m - (ITERS - 1) * chunks
         whole = prefix_v[m + chunks] + drift_v[m]
         out_v[c] = start_v[c] + whole.reshape(size, patches, features)
-        out_copy(c).start()
 
     chain(messages - 1)
     for m in range(messages - chunks + 1, messages):
@@ -412,15 +399,14 @@
         core_copy(m).wait_send()
         final_copy(m).wait_send()
         if columns == 2:
-            side_copy(m, chain_tx).wait_send()
+            for q in range(PIECES):
+                side_copy(m, chain_tx, q).wait_send()
 
     @pl.when(z < rows - 1)
     def _():
         for m in range(messages):
-            chain_copy(m).wait_send()
-
-    for c in range(chunks):
-        out_copy(c).wait()
+            for q in range(PIECES):
+                chain_copy(m, q).wait_send()
 
 
 def shards(
@@ -451,13 +437,13 @@
     matrix = jnp.asarray(group_matrix(channels, patches)).astype(BF16)
     smem = pl.BlockSpec(memory_space=pltpu.SMEM)
     vmem = pl.BlockSpec(memory_space=pltpu.VMEM)
-    anywhere = pl.BlockSpec(memory_space=pl.ANY)
+    anywhere = pl.BlockSpec(memory_space=pltpu.HBM)
     dma = pltpu.SemaphoreType.DMA
     out = pl.pallas_call(
         functools.partial(kernel, cfg),
-        out_shape=jax.ShapeDtypeStruct(chunked, F32),
+        out_shape=pltpu.VMEM(chunked, F32),
         in_specs=[smem, smem, vmem, vmem, vmem] + [anywhere] * 7,
-        out_specs=anywhere,
+        out_specs=vmem,
         scratch_shapes=[
             pltpu.VMEM(chunked, F32),
             pltpu.VMEM(chunked, F32),
@@ -477,13 +463,13 @@
             pltpu.VMEM(piece, F32),
             pltpu.VMEM(piece, F32),
             pltpu.VMEM((messages + chunks, 2, half, patches, features), F32),
-            pltpu.VMEM(chunked, F32),
             dma((7,)),
             dma((window,)),
             dma((window,)),
         ]
-        + [dma((messages,))] * 8
-        + [dma((chunks,))],
+        + [dma((messages,))] * 2
+        + [dma((messages, PIECES))] * 4
+        + [dma((messages,))] * 2,
         compiler_params=pltpu.CompilerParams(
             collective_id=0, has_side_effects=True, vmem_limit_bytes=56 * 1024 * 1024
         ),

time: 63.1 us -> 55.6 us (0.88)
  Pallas kernels: 59.5 us -> 53.2 us
  local copies, waits for them, and re-layouts: 2.07 us -> 0.88 us
    pallas_call x1, Pallas kernels: 59.5 us -> 53.2 us  [shards(): pl.pallas_call(functools.partial(kernel, cfg), out_shape=pltpu.VMEM(chunk...]
    unnamed x1, local copies, waits for them, and re-layouts: 2.07 us -> 0.88 us
where the time goes in v2:
time: 55.6 us; the launch traced here: 55.4 us
  Pallas kernels  53.2 us (96%)
  between operations  1.3 us (2%)
  local copies, waits for them, and re-layouts  0.88 us (2%)
    pallas_call x1, Pallas kernels, shards(): pl.pallas_call(functools.partial(kernel, cfg), out_shape=pltpu.VMEM(chunk...  53.2 us

profile of v2, /device:TPU:25, one launch (start us, length us, event | category | flops | bytes accessed | tf_op | source)
XLA Modules:
  0.0 55.4 jit_solution(300289314919938904)
XLA Ops:
  1.3 53.2 %shard_map.118 = f32[4,2,32,768]{3,2,1,0:T(8,128)S(1)} custom-call(s32[1]{0:T(128)S(6)} %copy.15.gap_ref, s32[1]{0:T(128)S(6)} %copy.16.start_level_ref, f32[8,128]{1,0:T(8,128)} %constant.6.clone.table_ref, f32[1,128]{1,0:T(1,128)} %constant.7.clone.freq_ref, bf16[256,256]{1,0:T(8,128)(2,1)} %constant.12.group_ref, f32[4,2,32,768]{3,2,1,0:T(8,128)} %bitcast.4, ...), custom_call_target="tpu_custom_call" | custom-call | tf_op jit(solution)/shard_map/pallas_call | solution.py:442
  54.5 0.9 %copy.14 = f32[1,8,32,768]{3,2,1,0:T(8,128)} copy(f32[1,8,32,768]{3,2,1,0:T(8,128)S(1)} %bitcast.3) | data formatting | bytes 1572864

commit v3 on v2

--- a/solution.py
+++ b/solution.py
@@ -10,7 +10,7 @@
 from jax.sharding import PartitionSpec as P
 
 GROUPS = 32
-PIECES = 2
+PIECES = 4
 ITERS = 2
 TRAIN_STEPS = 1000
 CHUNK_IMAGES = 2

time: 55.6 us -> 56.1 us (level)
  Pallas kernels: 53.2 us -> 53.8 us
where the time goes in v3:
time: 56.1 us; the launch traced here: 55.9 us
  Pallas kernels  53.8 us (96%)
  between operations  1.3 us (2%)
  local copies, waits for them, and re-layouts  0.88 us (2%)
    pallas_call x1, Pallas kernels, shards(): pl.pallas_call(functools.partial(kernel, cfg), out_shape=pltpu.VMEM(chunk...  53.8 us

profile of v3, /device:TPU:25, one launch (start us, length us, event | category | flops | bytes accessed | tf_op | source)
XLA Modules:
  0.0 55.9 jit_solution(1837241122047411012)
XLA Ops:
  1.3 53.8 %shard_map.118 = f32[4,2,32,768]{3,2,1,0:T(8,128)S(1)} custom-call(s32[1]{0:T(128)S(6)} %copy.15.gap_ref, s32[1]{0:T(128)S(6)} %copy.16.start_level_ref, f32[8,128]{1,0:T(8,128)} %constant.6.clone.table_ref, f32[1,128]{1,0:T(1,128)} %constant.7.clone.freq_ref, bf16[256,256]{1,0:T(8,128)(2,1)} %constant.12.group_ref, f32[4,2,32,768]{3,2,1,0:T(8,128)} %bitcast.4, ...), custom_call_target="tpu_custom_call" | custom-call | tf_op jit(solution)/shard_map/pallas_call | solution.py:442
  55.1 0.9 %copy.14 = f32[1,8,32,768]{3,2,1,0:T(8,128)} copy(f32[1,8,32,768]{3,2,1,0:T(8,128)S(1)} %bitcast.3) | data formatting | bytes 1572864

commit v4 on v2

--- a/solution.py
+++ b/solution.py
@@ -276,11 +276,9 @@
         rest = stacked - high.astype(F32)
         middle = rest.astype(BF16)
         low = (rest - middle.astype(F32)).astype(BF16)
-        summed = (
-            jnp.dot(low, matrix, preferred_element_type=F32)
-            + jnp.dot(middle, matrix, preferred_element_type=F32)
-            + jnp.dot(high, matrix, preferred_element_type=F32)
-        )
+        parts = jnp.concatenate([low, middle, high], axis=0)
+        summed = jnp.dot(parts, matrix, preferred_element_type=F32)
+        summed = jnp.sum(summed.reshape(3, -1, BLOCK), axis=0)
         summed = jnp.sum(summed.reshape(blocks, size, 8, BLOCK), axis=2, keepdims=True)
         return jnp.concatenate([summed[i] for i in range(blocks)], axis=-1)
 

time: 55.6 us -> 54.3 us (0.977)
  Pallas kernels: 53.2 us -> 52 us
    pallas_call x1, Pallas kernels: 53.2 us -> 52 us  [shards(): pl.pallas_call(functools.partial(kernel, cfg), out_shape=pltpu.VMEM(chunk...]
where the time goes in v4:
time: 54.3 us; the launch traced here: 54.2 us
  Pallas kernels  52 us (96%)
  between operations  1.3 us (2%)
  local copies, waits for them, and re-layouts  0.88 us (2%)
    pallas_call x1, Pallas kernels, shards(): pl.pallas_call(functools.partial(kernel, cfg), out_shape=pltpu.VMEM(chunk...  52 us

profile of v4, /device:TPU:25, one launch (start us, length us, event | category | flops | bytes accessed | tf_op | source)
XLA Modules:
  0.0 54.2 jit_solution(5047134572387963194)
XLA Ops:
  1.3 52.0 %shard_map.118 = f32[4,2,32,768]{3,2,1,0:T(8,128)S(1)} custom-call(s32[1]{0:T(128)S(6)} %copy.15.gap_ref, s32[1]{0:T(128)S(6)} %copy.16.start_level_ref, f32[8,128]{1,0:T(8,128)} %constant.6.clone.table_ref, f32[1,128]{1,0:T(1,128)} %constant.7.clone.freq_ref, bf16[256,256]{1,0:T(8,128)(2,1)} %constant.12.group_ref, f32[4,2,32,768]{3,2,1,0:T(8,128)} %bitcast.4, ...), custom_call_target="tpu_custom_call" | custom-call | tf_op jit(solution)/shard_map/pallas_call | solution.py:440
  53.3 0.9 %copy.14 = f32[1,8,32,768]{3,2,1,0:T(8,128)} copy(f32[1,8,32,768]{3,2,1,0:T(8,128)S(1)} %bitcast.3) | data formatting | bytes 1572864
